TPU v7x, 512 devices: a whole 4x4x16 slice. The times are simulated.
512 devices in a mesh: dp: 32 (over y_hi, z), mp: 16 (over x, y_lo, core).
Axes of the slice: x: 4, y: 4 (y_hi: 2, y_lo: 2; y = y_hi * 2 + y_lo), z: 16, core: 2. Of those that a mesh axis runs over, the one named last changes fastest.
Arguments:
- tokens: bfloat16 [32768, 4096], P('dp', 'mp'), may hold values from -6 to 6
- right_weight: bfloat16 [64, 64, 64], P('mp', 'dp'), may hold values from -0.75 to 0.75
- left_weight: bfloat16 [64, 64, 64], P('mp', 'dp'), may hold values from -0.75 to 0.75
- cotangent: bfloat16 [32768, 4096], P('dp', 'mp'), may hold values from -0.032958984 to 0.032958984
Outputs:
- activated: bfloat16 [32768, 4096], P('dp', 'mp')
- grad_right: float32 [64, 64, 64], P('mp', 'dp')
- grad_left: float32 [64, 64, 64], P('mp', 'dp')
All inputs are finite; a program needn't handle non-finite values.
Results may differ from a plain program's by a relative error of at most 0.0056.
Values may be sent and summed in bfloat16 or wider, within the bound.
A program may use at most 64 MiB of HBM per device.

v0:
```python
import jax
import jax.numpy as jnp
from jax import lax
from jax.sharding import PartitionSpec as P

NB = 64
BS = 64


def in_order(parts, dim):
    dims = list(parts.shape[1:])
    dims[dim] *= parts.shape[0]
    return jnp.moveaxis(parts, 0, dim).reshape(dims)


def gather_together(arrays, axis, dims):
    line = jnp.concatenate([a.reshape(-1) for a in arrays])
    lines, at, gathered = (lax.all_gather(line, axis), 0, [])
    for a, dim in zip(arrays, dims):
        parts = lines[:, at : at + a.size].reshape(-1, *a.shape)
        gathered.append(in_order(parts, dim))
        at += a.size
    return tuple(gathered)


def cut_along(x, dim, devices):
    before, after = (x.shape[:dim], x.shape[dim + 1 :])
    return jnp.moveaxis(x.reshape(*before, devices, -1, *after), dim, 0)


def sent_and_summed(x, axis, dim):
    devices = lax.axis_size(axis)
    parts = lax.all_to_all(cut_along(x, dim, devices), axis, 0, 0, tiled=True)
    return jnp.sum(parts, axis=0)


def in_one_piece(arrays, axis, dim, along):
    widths = [a.shape[along] for a in arrays]
    both = jnp.concatenate(arrays, axis=along)
    result = sent_and_summed(both, axis, dim)
    return tuple(jnp.split(result, [sum(widths[:k]) for k in range(1, len(widths))], axis=along))


def gelu_slope(pre):
    cdf = 0.5 * (1.0 + lax.erf(pre * 0.7071067811865476))
    density = jnp.exp(-0.5 * pre * pre) * 0.3989422804014327
    return cdf + pre * density


def shards(tokens, right_weight, left_weight, cotangent):
    tok_rows = tokens.shape[0]
    groups = lax.axis_size("mp")
    owned = NB // groups
    right_rows, left_rows = gather_together((right_weight, left_weight), "dp", (1, 1))
    xs = tokens.reshape(tok_rows, owned, BS)
    inner = jnp.einsum("tik,ikm->tmi", xs, right_rows, preferred_element_type=jnp.float32)
    inner = inner.astype(jnp.bfloat16).reshape(tok_rows, BS * owned)
    left_four = left_rows.reshape(owned, groups, owned, BS)
    received = lax.all_to_all(inner, "mp", split_axis=1, concat_axis=1, tiled=True)
    rows = received.shape[0]
    mixed = received.reshape(rows, groups, owned, owned)
    pre_rows = jnp.einsum("tpmj,mpjn->tmn", mixed, left_four, preferred_element_type=jnp.float32)
    received, pre = (received, pre_rows)
    mixed = received.reshape(tok_rows, groups, owned, owned)
    activated = (
        jax.nn.gelu(pre, approximate=False).astype(jnp.bfloat16).reshape(tok_rows, owned * BS)
    )
    dpre = (cotangent.reshape(tok_rows, owned, BS).astype(jnp.float32) * gelu_slope(pre)).astype(
        jnp.bfloat16
    )
    part_left = jnp.einsum("tpmj,tmn->mpjn", mixed, dpre, preferred_element_type=jnp.float32)
    part_left = part_left.reshape(owned, NB, BS)
    dmixed = jnp.einsum("tmn,mpjn->tpmj", dpre, left_four, preferred_element_type=jnp.float32)
    dmixed = dmixed.astype(jnp.bfloat16).reshape(tok_rows, groups * owned * owned)
    dinner = lax.all_to_all(dmixed, "mp", split_axis=1, concat_axis=1, tiled=True)
    dinner = dinner.reshape(tok_rows, groups, owned, owned)
    part_right = jnp.einsum("tik,tqmi->ikqm", xs, dinner, preferred_element_type=jnp.float32)
    part_right = part_right.reshape(owned, BS, BS)
    grad_right, grad_left = in_one_piece((part_right, part_left), "dp", 1, 0)
    return (activated, grad_right, grad_left)


def solution(mesh):
    return jax.shard_map(
        shards,
        mesh=mesh,
        in_specs=(P("dp", "mp"), P("mp", "dp", None), P("mp", "dp", None), P("dp", "mp")),
        out_specs=(P("dp", "mp"), P("mp", "dp", None), P("mp", "dp", None)),
        check_vma=False,
    )
```

profile of v0, /device:TPU:1, one launch (start us, length us, event | category | flops | bytes accessed | tf_op | source)
XLA Modules:
  0.0 150.1 jit_solution(9016281412636657445)
XLA Ops:
  0.6 0.8 reshape.55
  1.4 0.8 reshape.54
  2.2 69.5 %all-gather = bf16[32768]{0:T(1024)(128)(2,1)S(1)} all-gather(bf16[1024]{0:T(1024)(128)(2,1)S(1)} %pad_maximum_fusion), channel_id=2, replica_groups=mesh['dp'=32,'mp'=16] {'dp'}, dimensions={0}, use_global_device_ids=true | all-gather | bytes 67584 | tf_op jit(solution)/shard_map/all_gather | solution.py:18
  71.7 0.1 reshape.57
  71.8 1.2 copy.26
  73.1 0.0 copy-start
  73.1 0.3 fusion
  73.5 0.4 copy.28
  73.9 0.9 all_to_all.15
  74.8 19.3 %all-to-all-start = ((bf16[1024,16,16]{0,2,1:T(8,128)(2,1)}), bf16[1024,16,16]{0,2,1:T(8,128)(2,1)S(1)}, u32[]{:S(2)}, u32[]{:S(2)}) async-start(bf16[1024,16,16]{0,2,1:T(8,128)(2,1)} %all_to_all.15), calls=%async_computation | async-start | bytes 1048576 | tf_op jit(solution)/shard_map/all_to_all | solution.py:59
  94.1 0.0 copy-done
  94.1 0.2 copy.31
  94.3 0.1 reshape.56
  94.5 9.3 %all-to-all-done = bf16[1024,16,16]{0,2,1:T(8,128)(2,1)S(1)} async-done(((bf16[1024,16,16]{0,2,1:T(8,128)(2,1)}), bf16[1024,16,16]{0,2,1:T(8,128)(2,1)S(1)}, u32[]{:S(2)}, u32[]{:S(2)}) %all-to-all-start) | async-done | bytes 524320 | tf_op jit(solution)/shard_map/all_to_all | solution.py:59
  103.8 0.3 copy.29
  104.1 3.8 %fusion.9 = (bf16[1024,4,64]{0,2,1:T(8,128)(2,1)S(1)}, bf16[1024,4,64]{0,2,1:T(8,128)(2,1)}) fusion(f32[1024,4,64]{0,2,1:T(8,128)S(1)} %bitcast.50, bf16[1024,16,4,4]{0,1,3,2:T(8,128)(2,1)S(1)} %bitcast.47, bf16[4,16,4,64]{3,2,1,0:T(4,128)(2,1)S(1)} %bitcast.54), kind=kOutput, calls=%fused_computation.15 | convolution fusion | flops 53215232 | bytes 2654208 | tf_op jit(solution)/shard_map/tpmj,mpjn->tmn/dot_general | solution.py:62
  107.8 0.3 convolution_convert_fusion
  108.1 1.1 copy.33
  109.2 4.6 %all-to-all-start.1 = ((bf16[1024,16,16]{0,2,1:T(8,128)(2,1)}), bf16[1024,16,16]{0,2,1:T(8,128)(2,1)S(1)}, u32[]{:S(2)}, u32[]{:S(2)}) async-start(bf16[1024,16,16]{0,2,1:T(8,128)(2,1)} %copy.33), calls=%async_computation.1 | async-start | bytes 1048576 | tf_op jit(solution)/shard_map/all_to_all | solution.py:75
  113.8 0.3 fusion.17
  114.1 0.1 copy.37
  114.1 9.4 %all-to-all-done.1 = bf16[1024,16,16]{0,2,1:T(8,128)(2,1)S(1)} async-done(((bf16[1024,16,16]{0,2,1:T(8,128)(2,1)}), bf16[1024,16,16]{0,2,1:T(8,128)(2,1)S(1)}, u32[]{:S(2)}, u32[]{:S(2)}) %all-to-all-start.1) | async-done | bytes 524320 | tf_op jit(solution)/shard_map/all_to_all | solution.py:75
  123.5 0.3 copy.34
  123.8 0.3 convolution_bitcast_fusion.1
  124.1 1.0 copy.36
  125.1 0.0 copy-start.1
  125.1 1.0 concatenate.12
  126.2 0.1 maximum_bitcast_fusion
  126.3 0.1 copy.38
  126.4 0.9 reshape.68
  127.3 3.9 %all-to-all-start.2 = ((f32[32,1,1024]{2,1,0:T(1,128)}), f32[32,1,1024]{2,1,0:T(1,128)S(1)}, u32[]{:S(2)}, u32[]{:S(2)}) async-start(f32[32,1,1024]{2,1,0:T(1,128)} %reshape.68), calls=%async_computation.2 | async-start | bytes 262144 | tf_op jit(solution)/shard_map/all_to_all | solution.py:33
  131.2 0.0 copy-done.1
  131.2 1.0 copy.39
  132.2 15.5 %all-to-all-done.2 = f32[32,1,1024]{2,1,0:T(1,128)S(1)} async-done(((f32[32,1,1024]{2,1,0:T(1,128)}), f32[32,1,1024]{2,1,0:T(1,128)S(1)}, u32[]{:S(2)}, u32[]{:S(2)}) %all-to-all-start.2) | async-done | bytes 131104 | tf_op jit(solution)/shard_map/all_to_all | solution.py:33
  147.7 0.5 broadcast.18
  148.2 0.9 reduce
  149.2 0.2 reshape.69
  149.4 0.1 reduce_sum.9
  149.5 0.6 fusion.24
  (5 shorter events, 0.1 us)
Async XLA Ops:
  73.1 21.0 %copy-start = (bf16[1024,256]{1,0:T(8,128)(2,1)S(1)}, bf16[1024,256]{1,0:T(8,128)(2,1)}, u32[]{:S(2)}) copy-start(bf16[1024,256]{1,0:T(8,128)(2,1)} %param.7) | copy-start | bytes 1572868
  74.8 29.0 %all-to-all-start = ((bf16[1024,16,16]{0,2,1:T(8,128)(2,1)}), bf16[1024,16,16]{0,2,1:T(8,128)(2,1)S(1)}, u32[]{:S(2)}, u32[]{:S(2)}) async-start(bf16[1024,16,16]{0,2,1:T(8,128)(2,1)} %all_to_all.15), calls=%async_computation | async-start | bytes 1048576 | tf_op jit(solution)/shard_map/all_to_all | solution.py:59
  109.2 14.3 %all-to-all-start.1 = ((bf16[1024,16,16]{0,2,1:T(8,128)(2,1)}), bf16[1024,16,16]{0,2,1:T(8,128)(2,1)S(1)}, u32[]{:S(2)}, u32[]{:S(2)}) async-start(bf16[1024,16,16]{0,2,1:T(8,128)(2,1)} %copy.33), calls=%async_computation.1 | async-start | bytes 1048576 | tf_op jit(solution)/shard_map/all_to_all | solution.py:75
  125.1 6.1 %copy-start.1 = (bf16[1024,4,64]{0,2,1:T(8,128)(2,1)S(1)}, bf16[1024,4,64]{0,2,1:T(8,128)(2,1)}, u32[]{:S(2)}) copy-start(bf16[1024,4,64]{0,2,1:T(8,128)(2,1)} %get-tuple-element.13) | copy-start | bytes 1572868
  127.3 20.4 %all-to-all-start.2 = ((f32[32,1,1024]{2,1,0:T(1,128)}), f32[32,1,1024]{2,1,0:T(1,128)S(1)}, u32[]{:S(2)}, u32[]{:S(2)}) async-start(f32[32,1,1024]{2,1,0:T(1,128)} %reshape.68), calls=%async_computation.2 | async-start | bytes 262144 | tf_op jit(solution)/shard_map/all_to_all | solution.py:33
where the time goes:
time: 152 us; the launch traced here: 150 us
  blocking collectives  69.5 us (46%)
  waiting for transfers between devices  34.2 us (23%)
  starting transfers between devices  27.7 us (18%)
  local copies, waits for them, and re-layouts  11.7 us (8%)
  matrix products  4.94 us (3%)
    all_gather x1, blocking collectives, gather_together(): lines, at, gathered = (lax.all_gather(line, axis), 0, [])  69.5 us
    all_to_all x1, starting transfers between devices, shards(): lax.all_to_all(inner, 'mp', split_axis=1, concat_axis=1, tiled=True)  19.3 us
    all_to_all x1, waiting for transfers between devices, sent_and_summed(): parts = lax.all_to_all(cut_along(x, dim, devices), axis, 0, 0, tiled=True)  15.5 us
    all_to_all x1, waiting for transfers between devices, shards(): lax.all_to_all(dmixed, 'mp', split_axis=1, concat_axis=1, tiled=True)  9.41 us
    all_to_all x1, waiting for transfers between devices, shards(): lax.all_to_all(inner, 'mp', split_axis=1, concat_axis=1, tiled=True)  9.32 us
    all_to_all x1, starting transfers between devices, shards(): lax.all_to_all(dmixed, 'mp', split_axis=1, concat_axis=1, tiled=True)  4.58 us
    all_to_all x1, starting transfers between devices, sent_and_summed(): parts = lax.all_to_all(cut_along(x, dim, devices), axis, 0, 0, tiled=True)  3.86 us
    dot_general x1, matrix products, shards(): jnp.einsum('tpmj,mpjn->tmn', mixed, left_four, preferred_element_type=jnp...  3.76 us
  transfers between devices with their start and end apart: 3, of which 3 were waited for; matrix products, arithmetic and copies ran while one was open for 1% of the time, Pallas kernels for 0%

commit v1 on v0

v1 whole, which is shorter than its diff:
```python
import functools

import jax
import jax.numpy as jnp
from jax import lax
from jax.experimental import pallas as pl
from jax.experimental.pallas import tpu as pltpu
from jax.sharding import PartitionSpec as P

MESH = pl.DeviceIdType.MESH
BF = jnp.bfloat16
F32 = jnp.float32
CHUNK = 256


def iota(dim, shape=(256, 256)):
    return lax.broadcasted_iota(jnp.int32, shape, dim)


def nn(a, b):
    return lax.dot_general(a, b, (((1,), (0,)), ((), ())), preferred_element_type=F32)


def nt(a, b):
    return lax.dot_general(a, b, (((1,), (1,)), ((), ())), preferred_element_type=F32)


def ones_where(cond):
    return jnp.where(cond, 1.0, 0.0).astype(BF)


def diagonal_blocks(full):
    lane = iota(1, (64, 256)) // 64
    total = jnp.zeros((64, 256), F32)
    for b in range(4):
        total = jnp.where(lane == b, full[64 * b : 64 * b + 64], total)
    return total


def kernel(
    n_dp,
    n_mp,
    x_hbm,
    rw_hbm,
    lw_hbm,
    cot_hbm,
    act_hbm,
    gr_ref,
    gl_ref,
    x_v,
    cot_v,
    rw_v,
    lw_v,
    xt_v,
    cott_v,
    s1_v,
    r_v,
    s2_v,
    d_v,
    actt_v,
    act_v,
    send_rw,
    send_lw,
    got_rw,
    got_lw,
    kr_v,
    kl_v,
    got_kr,
    got_kl,
    in_sem,
    out_sem,
    w_send,
    w_recv,
    a_send,
    a_recv,
    g_send,
    g_recv,
):
    tok = x_v.shape[0]
    chunks = tok // CHUNK
    dp = lax.axis_index("dp")
    mp = lax.axis_index("mp")
    n_z = n_dp // 2

    def dp_peer(t):
        o = t // 2
        step = (o + 1) // 2
        zoff = n_z // 2 + jnp.where(o % 2 == 1, -step, step)
        z = lax.rem(lax.rem(dp, n_z) + zoff + n_z, n_z)
        y = lax.rem(dp // n_z + 1 + lax.rem(t, 2), 2)
        return y * n_z + z

    def mp_peer(j):
        return lax.rem(mp + j, n_mp)

    loads = [
        pltpu.make_async_copy(rw_hbm, rw_v, in_sem.at[0]),
        pltpu.make_async_copy(lw_hbm, lw_v, in_sem.at[1]),
        pltpu.make_async_copy(x_hbm, x_v, in_sem.at[2]),
        pltpu.make_async_copy(cot_hbm, cot_v, in_sem.at[3]),
    ]
    for load in loads:
        load.start()

    barrier = pltpu.get_barrier_semaphore()

    @pl.loop(0, n_dp - 1)
    def _(t):
        pl.semaphore_signal(barrier, inc=1, device_id={"dp": dp_peer(t)}, device_id_type=MESH)

    @pl.loop(1, n_mp)
    def _(j):
        pl.semaphore_signal(barrier, inc=1, device_id={"mp": mp_peer(j)}, device_id_type=MESH)

    loads[0].wait()
    loads[1].wait()
    mine_r = jnp.concatenate([rw_v[i].astype(F32) for i in range(4)], axis=1).astype(BF)
    mine_l = jnp.concatenate([lw_v[i].astype(F32) for i in range(4)], axis=1).astype(BF)
    send_rw[...] = mine_r
    send_lw[...] = mine_l
    got_rw[dp] = mine_r
    got_lw[dp] = mine_l

    pl.semaphore_wait(barrier, n_dp - 1 + n_mp - 1)

    for k, (src, dst) in enumerate(((send_rw, got_rw), (send_lw, got_lw))):

        @pl.loop(0, n_dp - 1)
        def _(t):
            pltpu.make_async_remote_copy(
                src_ref=src,
                dst_ref=dst.at[dp],
                send_sem=w_send.at[k],
                recv_sem=w_recv.at[k],
                device_id={"dp": dp_peer(t)},
                device_id_type=MESH,
            ).start()

    loads[2].wait()
    loads[3].wait()
    xt_v[...] = x_v[...].T
    cott_v[...] = cot_v[...].T

    row, col = iota(0), iota(1)
    to_r = ones_where(col == (row % 4) * 64 + row // 4)
    from_r = ones_where(row == (col % 4) * 64 + col // 4)
    rep = ones_where(iota(1, (256, 64)) == (iota(0, (256, 64)) // 16) * 4 + iota(0, (256, 64)) % 4)

    others = got_rw.at[pl.ds(0, n_dp - 1)]
    pltpu.make_async_copy(others, others, w_recv.at[0]).wait()
    rows = got_rw[...].reshape(64, 256).astype(F32)
    lane = iota(1, (64, 256)) // 64
    block_diag = jnp.concatenate([jnp.where(lane == b, rows, 0.0) for b in range(4)], axis=0).astype(BF)
    first = nt(to_r, block_diag).astype(BF)

    def exchange(c, src, dst, k):
        mine = pl.ds(pl.multiple_of(16 * mp, 16), 16)

        @pl.loop(1, n_mp)
        def _(j):
            q = mp_peer(j)
            pltpu.make_async_remote_copy(
                src_ref=src.at[c, pl.ds(pl.multiple_of(16 * q, 16), 16), :],
                dst_ref=dst.at[c, mine, :],
                send_sem=a_send.at[k, c],
                recv_sem=a_recv.at[k, c],
                device_id={"mp": q},
                device_id_type=MESH,
            ).start()

        dst[c, mine, :] = src[c, mine, :]

    def arrived(dst, c, k):
        others = dst.at[c, pl.ds(0, 16 * (n_mp - 1)), :]
        pltpu.make_async_copy(others, others, a_recv.at[k, c]).wait()

    for c in range(chunks):
        s1_v[c] = nn(first, xt_v[:, CHUNK * c : CHUNK * (c + 1)]).astype(BF)
        exchange(c, s1_v, r_v, 0)

    others_l = got_lw.at[pl.ds(0, n_dp - 1)]
    pltpu.make_async_copy(others_l, others_l, w_recv.at[1]).wait()
    spread = nn(rep, got_lw[...].reshape(64, 256))
    second_f = jnp.where(col // 64 == (row // 4) % 4, spread, 0.0)
    second = second_f.astype(BF)
    second_t = second_f.T.astype(BF)

    left = jnp.zeros((256, 256), F32)
    for c in range(chunks):
        arrived(r_v, c, 0)
        inner = r_v[c]
        pre = nn(second_t, inner)
        cdf = 0.5 * (1.0 + lax.erf(pre * 0.7071067811865476))
        density = jnp.exp(-0.5 * pre * pre) * 0.3989422804014327
        cot = cott_v[:, CHUNK * c : CHUNK * (c + 1)].astype(F32)
        dpre = (cot * (cdf + pre * density)).astype(BF)
        s2_v[c] = nn(second, dpre).astype(BF)
        exchange(c, s2_v, d_v, 1)
        actt_v[:, CHUNK * c : CHUNK * (c + 1)] = (pre * cdf).astype(BF)
        left = left + nt(inner, dpre)

    def scatter(src, dst, k):
        @pl.loop(0, n_dp - 1)
        def _(t):
            peer = dp_peer(t)
            pltpu.make_async_remote_copy(
                src_ref=src.at[peer],
                dst_ref=dst.at[dp],
                send_sem=g_send.at[k],
                recv_sem=g_recv.at[k],
                device_id={"dp": peer},
                device_id_type=MESH,
            ).start()

        dst[dp] = src[dp]

    def collect(dst, k):
        others = dst.at[pl.ds(0, n_dp - 1)]
        pltpu.make_async_copy(others, others, g_recv.at[k]).wait()
        return jnp.sum(dst[...], axis=0)

    left = jnp.where(col // 64 == (row // 4) % 4, left, 0.0)
    left = jnp.sum(left.reshape(16, 4, 4, 256), axis=1)
    kl_v[...] = left.reshape(n_dp, 2, 256)
    scatter(kl_v, got_kl, 0)

    right = jnp.zeros((256, 256), F32)
    for c in range(chunks):
        arrived(d_v, c, 1)
        dinner = nn(from_r, d_v[c]).astype(BF)
        right = right + nt(xt_v[:, CHUNK * c : CHUNK * (c + 1)], dinner)
    kr_v[...] = diagonal_blocks(right).reshape(n_dp, 2, 256)
    scatter(kr_v, got_kr, 1)

    act_v[...] = actt_v[...].T
    store = pltpu.make_async_copy(act_v, act_hbm, out_sem)
    store.start()

    sum_l = collect(got_kl, 0)
    for b in range(4):
        gl_ref[b] = sum_l[:, 64 * b : 64 * b + 64]
    sum_r = collect(got_kr, 1)
    for b in range(4):
        gr_ref[b] = sum_r[:, 64 * b : 64 * b + 64]

    for k, dst in enumerate((got_rw, got_lw)):
        sent = dst.at[pl.ds(0, n_dp - 1)]
        pltpu.make_async_copy(sent, sent, w_send.at[k]).wait()
    for k, src in enumerate((s1_v, s2_v)):
        for c in range(chunks):
            sent = src.at[c, pl.ds(0, 16 * (n_mp - 1)), :]
            pltpu.make_async_copy(sent, sent, a_send.at[k, c]).wait()
    for k, src in enumerate((kl_v, kr_v)):
        sent = src.at[pl.ds(0, n_dp - 1)]
        pltpu.make_async_copy(sent, sent, g_send.at[k]).wait()
    store.wait()


def shards(n_dp, n_mp, tokens, right_weight, left_weight, cotangent):
    tok = tokens.shape[0]
    chunks = tok // CHUNK
    vmem, sem = pltpu.VMEM, pltpu.SemaphoreType.DMA
    any_space = pl.BlockSpec(memory_space=pl.ANY)
    in_vmem = pl.BlockSpec(memory_space=pltpu.VMEM)
    activated, grad_right, grad_left = pl.pallas_call(
        functools.partial(kernel, n_dp, n_mp),
        out_shape=[
            jax.ShapeDtypeStruct((tok, 256), BF),
            jax.ShapeDtypeStruct((4, 2, 64), F32),
            jax.ShapeDtypeStruct((4, 2, 64), F32),
        ],
        in_specs=[any_space] * 4,
        out_specs=[any_space, in_vmem, in_vmem],
        scratch_shapes=[
            vmem((tok, 256), BF),
            vmem((tok, 256), BF),
            vmem((4, 2, 64), BF),
            vmem((4, 2, 64), BF),
            vmem((256, tok), BF),
            vmem((256, tok), BF),
            vmem((chunks, 256, CHUNK), BF),
            vmem((chunks, 256, CHUNK), BF),
            vmem((chunks, 256, CHUNK), BF),
            vmem((chunks, 256, CHUNK), BF),
            vmem((256, tok), BF),
            vmem((tok, 256), BF),
            vmem((2, 256), BF),
            vmem((2, 256), BF),
            vmem((n_dp, 2, 256), BF),
            vmem((n_dp, 2, 256), BF),
            vmem((n_dp, 2, 256), F32),
            vmem((n_dp, 2, 256), F32),
            vmem((n_dp, 2, 256), F32),
            vmem((n_dp, 2, 256), F32),
            sem((4,)),
            sem,
            sem((2,)),
            sem((2,)),
            sem((2, chunks)),
            sem((2, chunks)),
            sem((2,)),
            sem((2,)),
        ],
        compiler_params=pltpu.CompilerParams(collective_id=0, has_side_effects=True),
        name="monarch",
    )(tokens, right_weight, left_weight, cotangent)
    return activated, grad_right, grad_left


def solution(mesh):
    return jax.shard_map(
        functools.partial(shards, mesh.shape["dp"], mesh.shape["mp"]),
        mesh=mesh,
        in_specs=(P("dp", "mp"), P("mp", "dp", None), P("mp", "dp", None), P("dp", "mp")),
        out_specs=(P("dp", "mp"), P("mp", "dp", None), P("mp", "dp", None)),
        check_vma=False,
    )
```

time: 152 us -> 54.4 us (0.36); the launches traced: 150 us -> 54.3 us
  blocking collectives: 69.5 us -> 0 us
  Pallas kernels: 0 us -> 50.5 us
  waiting for transfers between devices: 34.2 us -> 0 us
  starting transfers between devices: 27.7 us -> 0 us
  local copies, waits for them, and re-layouts: 11.7 us -> 3.15 us
  matrix products: 4.94 us -> 0 us
    all_gather x1 -> x0, blocking collectives: 69.5 us -> none  [gather_together(): lines, at, gathered = (lax.all_gather(line, axis), 0, [])]
    pallas_call x0 -> x1, Pallas kernels: none -> 50.5 us  [shards(): pl.pallas_call(functools.partial(kernel, n_dp, n_mp), out_shape=[jax.Shap...]
    all_to_all x3 -> x0, waiting for transfers between devices: 34.2 us -> none  [the longest x1 15.5 us: sent_and_summed(): parts = lax.all_to_all(cut_along(x, dim, devices), axis, 0, 0, tiled=True)]
    all_to_all x3 -> x0, starting transfers between devices: 27.7 us -> none  [the longest x1 19.3 us: shards(): lax.all_to_all(inner, 'mp', split_axis=1, concat_axis=1, tiled=True)]
    dot_general x5 -> x0, matrix products: 4.94 us -> none  [the longest x1 3.76 us: shards(): jnp.einsum('tpmj,mpjn->tmn', mixed, left_four, preferred_element_type=jnp...]
    all_to_all x5 -> x0, local copies, waits for them, and re-layouts: 3.09 us -> none  [the longest x2 1.37 us: shards(): lax.all_to_all(dmixed, 'mp', split_axis=1, concat_axis=1, tiled=True)]
    reshape x5 -> x0, local copies, waits for them, and re-layouts: 1.78 us -> none  [the longest x2 1.53 us: gather_together(): line = jnp.concatenate([a.reshape(-1) for a in arrays])]
    unnamed x8 -> x7, local copies, waits for them, and re-layouts: 3.37 us -> 3.15 us
  transfers between devices with their start and end apart: 3 -> 0, of which waited for: 3 -> 0; matrix products, arithmetic and copies ran while one was open for 1% -> 0% of each run, Pallas kernels for 0% -> 0%
where the time goes in v1:
time: 54.4 us; the launch traced here: 54.3 us
  Pallas kernels  50.5 us (93%)
  local copies, waits for them, and re-layouts  3.15 us (6%)
  between operations  0.65 us (1%)
    pallas_call x1, Pallas kernels, shards(): pl.pallas_call(functools.partial(kernel, n_dp, n_mp), out_shape=[jax.Shap...  50.5 us
    unnamed x7, local copies, waits for them, and re-layouts  3.15 us

profile of v1, /device:TPU:1, one launch (start us, length us, event | category | flops | bytes accessed | tf_op | source)
XLA Modules:
  0.0 54.3 jit_solution(13677287413990875916)
XLA Ops:
  0.6 50.5 %monarch.1 = (bf16[1024,256]{1,0:T(8,128)(2,1)}, f32[4,2,64]{2,1,0:T(2,128)}, f32[4,2,64]{2,1,0:T(2,128)}) custom-call(bf16[1024,256]{1,0:T(8,128)(2,1)} %x_hbm.1, bf16[4,2,64]{2,1,0:T(2,128)(2,1)} %rw_hbm.1, bf16[4,2,64]{2,1,0:T(2,128)(2,1)} %lw_hbm.1, bf16[1024,256]{1,0:T(8,128)(2,1)} %cot_hbm.1), custom_call_target="tpu_custom_call" | custom-call | tf_op jit(solution)/shard_map/monarch/pallas_call | solution.py:265
  51.1 0.0 copy-start.1
  51.1 1.9 %copy.10 = bf16[1024,256]{1,0:T(8,128)(2,1)} copy(bf16[1024,256]{1,0:T(8,128)(2,1)} %get-tuple-element.6) | data formatting | bytes 1048576
  53.0 0.0 copy-done.1
  53.0 0.0 copy-start
  53.0 0.6 %copy.11 = f32[4,2,64]{2,1,0:T(2,128)} copy(f32[4,2,64]{2,1,0:T(2,128)S(1)} %copy-done.1) | data formatting | bytes 4096
  53.6 0.1 copy-done
  53.7 0.6 %copy.12 = f32[4,2,64]{2,1,0:T(2,128)} copy(f32[4,2,64]{2,1,0:T(2,128)S(1)} %copy-done) | data formatting | bytes 4096
Async XLA Ops:
  51.1 1.9 %copy-start.1 = (f32[4,2,64]{2,1,0:T(2,128)S(1)}, f32[4,2,64]{2,1,0:T(2,128)}, u32[]{:S(2)}) copy-start(f32[4,2,64]{2,1,0:T(2,128)} %get-tuple-element.7) | copy-start | bytes 6148
  53.0 0.7 %copy-start = (f32[4,2,64]{2,1,0:T(2,128)S(1)}, f32[4,2,64]{2,1,0:T(2,128)}, u32[]{:S(2)}) copy-start(f32[4,2,64]{2,1,0:T(2,128)} %get-tuple-element.8) | copy-start | bytes 6148

commit v2 on v1

v2 whole, which is shorter than its diff:
```python
import functools

import jax
import jax.numpy as jnp
from jax import lax
from jax.experimental import pallas as pl
from jax.experimental.pallas import tpu as pltpu
from jax.sharding import PartitionSpec as P

MESH = pl.DeviceIdType.MESH
BF = jnp.bfloat16
F32 = jnp.float32
CHUNK = 256
N_Z = 16
N_X = 4
NEAR = [(dz, dy) for dz in (-3, 2, -2, 1, -1, 0) for dy in (1, 0) if (dz, dy) != (0, 0)]
FAR = 5
FORWARD = [(-FAR, b) for b in (3, 2, 1, 0, -1)] + [(FAR, b) for b in (-2, -1, 0, 1, 2)]
FORWARD = [FORWARD[i + 5 * s] for i in range(5) for s in range(2)]
ALL_DP = [(dz, dy) for dz in (8, 7, -7, 6, -6, 5, -5, 4, -4, 3, -3, 2, -2, 1, -1, 0) for dy in (1, 0) if (dz, dy) != (0, 0)]
ALL_MP = [(dx, dy, dc) for dx in (2, 1, 3, 0) for dy in (1, 0) for dc in (1, 0) if (dx, dy, dc) != (0, 0, 0)]


def iota(dim, shape=(256, 256)):
    return lax.broadcasted_iota(jnp.int32, shape, dim)


def nn(a, b):
    return lax.dot_general(a, b, (((1,), (0,)), ((), ())), preferred_element_type=F32)


def nt(a, b):
    return lax.dot_general(a, b, (((1,), (1,)), ((), ())), preferred_element_type=F32)


def ones_where(cond):
    return jnp.where(cond, 1.0, 0.0).astype(BF)


def wrap(v, n):
    v = jnp.where(v >= n, v - n, v)
    return jnp.where(v < 0, v + n, v)


def diagonal_blocks(full):
    lane = iota(1, (64, 256)) // 64
    total = full[:64]
    for b in range(1, 4):
        total = jnp.where(lane == b, full[64 * b : 64 * b + 64], total)
    return total


def kernel(
    x_hbm,
    rw_hbm,
    lw_hbm,
    cot_hbm,
    act_ref,
    gr_ref,
    gl_ref,
    x_v,
    cot_v,
    rw_v,
    lw_v,
    xt_v,
    cott_v,
    s1_v,
    r_v,
    s2_v,
    d_v,
    actt_v,
    got_rw,
    got_lw,
    kr_v,
    kl_v,
    got_kr,
    got_kl,
    in_sem,
    w_send,
    w_recv,
    a_send,
    a_recv,
    g_send,
    g_recv,
):
    tok = x_v.shape[0]
    chunks = tok // CHUNK
    n_dp, n_mp = 2 * N_Z, 4 * N_X
    dp = lax.axis_index("dp")
    mp = lax.axis_index("mp")
    y = dp // N_Z
    z = dp - y * N_Z
    core = lax.rem(mp, 2)
    y_lo = lax.rem(mp // 2, 2)
    x = mp // 4

    def dp_peer(dz, dy):
        return (1 - y if dy else y) * N_Z + wrap(z + dz, N_Z)

    def mp_peer(dx, dy, dc):
        return wrap(x + dx, N_X) * 4 + (1 - y_lo if dy else y_lo) * 2 + (1 - core if dc else core)

    barrier = pltpu.get_barrier_semaphore()
    greet = [(FAR, 0), (-FAR, 0)] + [(-dz, dy) for dz, dy in NEAR]
    for dz, dy in greet:
        pl.semaphore_signal(barrier, inc=1, device_id={"dp": dp_peer(dz, dy)}, device_id_type=MESH)
    for d in ALL_MP:
        pl.semaphore_signal(barrier, inc=1, device_id={"mp": mp_peer(*d)}, device_id_type=MESH)

    loads = [
        pltpu.make_async_copy(rw_hbm, rw_v, in_sem.at[0]),
        pltpu.make_async_copy(lw_hbm, lw_v, in_sem.at[1]),
        pltpu.make_async_copy(x_hbm, x_v, in_sem.at[2]),
        pltpu.make_async_copy(cot_hbm, cot_v, in_sem.at[3]),
    ]
    for load in loads:
        load.start()

    loads[0].wait()
    loads[1].wait()
    got_rw[y, z] = jnp.concatenate([rw_v[i].astype(F32) for i in range(4)], axis=1).astype(BF)
    got_lw[y, z] = jnp.concatenate([lw_v[i].astype(F32) for i in range(4)], axis=1).astype(BF)
    loads[2].wait()
    loads[3].wait()
    xt_v[...] = x_v[...].T
    cott_v[...] = cot_v[...].T

    pl.semaphore_wait(barrier, len(greet) + len(ALL_MP))

    gathers = (got_rw, got_lw)
    for k, got in enumerate(gathers):
        for dz, dy in NEAR:
            pltpu.make_async_remote_copy(
                src_ref=got.at[y, z],
                dst_ref=got.at[y, z],
                send_sem=w_send.at[k, 0],
                recv_sem=w_recv.at[k, 0],
                device_id={"dp": dp_peer(dz, dy)},
                device_id_type=MESH,
            ).start()

    row, col = iota(0), iota(1)
    to_r = ones_where(col == (row % 4) * 64 + row // 4)
    from_r = ones_where(row == (col % 4) * 64 + col // 4)
    rep = ones_where(iota(1, (256, 64)) == (iota(0, (256, 64)) // 16) * 4 + iota(0, (256, 64)) % 4)

    def near_blocks(k):
        return gathers[k].at[0, pl.ds(0, len(NEAR))]

    def far_blocks(k):
        return gathers[k].at[:, pl.ds(0, len(FORWARD))]

    for k, got in enumerate(gathers):
        pltpu.make_async_copy(near_blocks(k), near_blocks(k), w_recv.at[k, 0]).wait()
        for dz, b in FORWARD:
            blocks = got.at[:, wrap(z + b, N_Z)]
            pltpu.make_async_remote_copy(
                src_ref=blocks,
                dst_ref=blocks,
                send_sem=w_send.at[k, 1],
                recv_sem=w_recv.at[k, 1],
                device_id={"dp": dp_peer(dz, 0)},
                device_id_type=MESH,
            ).start()

    pltpu.make_async_copy(far_blocks(0), far_blocks(0), w_recv.at[0, 1]).wait()
    rows = got_rw[...].reshape(64, 256).astype(F32)
    lane = iota(1, (64, 256)) // 64
    block_diag = jnp.concatenate([jnp.where(lane == b, rows, 0.0) for b in range(4)], axis=0).astype(BF)
    first = nt(to_r, block_diag).astype(BF)

    mine = pl.ds(pl.multiple_of(16 * mp, 16), 16)

    def exchange(c, src, dst, k):
        for d in ALL_MP:
            q = mp_peer(*d)
            pltpu.make_async_remote_copy(
                src_ref=src.at[c, pl.ds(pl.multiple_of(16 * q, 16), 16), :],
                dst_ref=dst.at[c, mine, :],
                send_sem=a_send.at[k, c],
                recv_sem=a_recv.at[k, c],
                device_id={"mp": q},
                device_id_type=MESH,
            ).start()
        dst[c, mine, :] = src[c, mine, :]

    def arrived(dst, c, k):
        others = dst.at[c, pl.ds(0, 16 * (n_mp - 1)), :]
        pltpu.make_async_copy(others, others, a_recv.at[k, c]).wait()

    for c in range(chunks):
        s1_v[c] = nn(first, xt_v[:, CHUNK * c : CHUNK * (c + 1)]).astype(BF)
        exchange(c, s1_v, r_v, 0)

    pltpu.make_async_copy(far_blocks(1), far_blocks(1), w_recv.at[1, 1]).wait()
    spread = nn(rep, got_lw[...].reshape(64, 256))
    second_f = jnp.where(col // 64 == (row // 4) % 4, spread, 0.0)
    second = second_f.astype(BF)
    second_t = second_f.T.astype(BF)

    left = jnp.zeros((256, 256), F32)
    for c in range(chunks):
        arrived(r_v, c, 0)
        inner = r_v[c]
        pre = nn(second_t, inner)
        cdf = 0.5 * (1.0 + lax.erf(pre * 0.7071067811865476))
        density = jnp.exp(-0.5 * pre * pre) * 0.3989422804014327
        cot = cott_v[:, CHUNK * c : CHUNK * (c + 1)].astype(F32)
        dpre = (cot * (cdf + pre * density)).astype(BF)
        s2_v[c] = nn(second, dpre).astype(BF)
        exchange(c, s2_v, d_v, 1)
        actt_v[:, CHUNK * c : CHUNK * (c + 1)] = (pre * cdf).astype(BF)
        left = left + nt(inner, dpre)

    def scatter(src, dst, k):
        for d in ALL_DP:
            peer = dp_peer(*d)
            pltpu.make_async_remote_copy(
                src_ref=src.at[peer],
                dst_ref=dst.at[dp],
                send_sem=g_send.at[k],
                recv_sem=g_recv.at[k],
                device_id={"dp": peer},
                device_id_type=MESH,
            ).start()
        dst[dp] = src[dp]

    def collect(dst, k):
        others = dst.at[pl.ds(0, n_dp - 1)]
        pltpu.make_async_copy(others, others, g_recv.at[k]).wait()
        return jnp.sum(dst[...], axis=0)

    left = jnp.where(col // 64 == (row // 4) % 4, left, 0.0)
    left = jnp.sum(left.reshape(16, 4, 4, 256), axis=1)
    kl_v[...] = left.reshape(n_dp, 2, 256)
    scatter(kl_v, got_kl, 0)

    right = jnp.zeros((256, 256), F32)
    for c in range(chunks):
        arrived(d_v, c, 1)
        dinner = nn(from_r, d_v[c]).astype(BF)
        right = right + nt(xt_v[:, CHUNK * c : CHUNK * (c + 1)], dinner)
    kr_v[...] = diagonal_blocks(right).reshape(n_dp, 2, 256)
    scatter(kr_v, got_kr, 1)

    act_ref[...] = actt_v[...].T

    sum_l = collect(got_kl, 0)
    for b in range(4):
        gl_ref[b] = sum_l[:, 64 * b : 64 * b + 64]
    for k in range(2):
        pltpu.make_async_copy(near_blocks(k), near_blocks(k), w_send.at[k, 0]).wait()
        pltpu.make_async_copy(far_blocks(k), far_blocks(k), w_send.at[k, 1]).wait()
    for k, src in enumerate((s1_v, s2_v)):
        for c in range(chunks):
            sent = src.at[c, pl.ds(0, 16 * (n_mp - 1)), :]
            pltpu.make_async_copy(sent, sent, a_send.at[k, c]).wait()
    for k, src in enumerate((kl_v, kr_v)):
        sent = src.at[pl.ds(0, n_dp - 1)]
        pltpu.make_async_copy(sent, sent, g_send.at[k]).wait()
    sum_r = collect(got_kr, 1)
    for b in range(4):
        gr_ref[b] = sum_r[:, 64 * b : 64 * b + 64]


def write_out(act, gr, gl, act_hbm, gr_hbm, gl_hbm, sem):
    copies = [
        pltpu.make_async_copy(src, dst, sem.at[k])
        for k, (src, dst) in enumerate(((act, act_hbm), (gr, gr_hbm), (gl, gl_hbm)))
    ]
    for copy in copies:
        copy.start()
    for copy in copies:
        copy.wait()


def shards(tokens, right_weight, left_weight, cotangent):
    tok = tokens.shape[0]
    chunks = tok // CHUNK
    n_dp = 2 * N_Z
    vmem, sem = pltpu.VMEM, pltpu.SemaphoreType.DMA
    any_space = pl.BlockSpec(memory_space=pl.ANY)
    in_vmem = pl.BlockSpec(memory_space=pltpu.VMEM)
    shapes = [((tok, 256), BF), ((4, 2, 64), F32), ((4, 2, 64), F32)]
    results = pl.pallas_call(
        kernel,
        out_shape=[pltpu.VMEM(*s) for s in shapes],
        in_specs=[any_space] * 4,
        out_specs=[in_vmem] * 3,
        scratch_shapes=[
            vmem((tok, 256), BF),
            vmem((tok, 256), BF),
            vmem((4, 2, 64), BF),
            vmem((4, 2, 64), BF),
            vmem((256, tok), BF),
            vmem((256, tok), BF),
            vmem((chunks, 256, CHUNK), BF),
            vmem((chunks, 256, CHUNK), BF),
            vmem((chunks, 256, CHUNK), BF),
            vmem((chunks, 256, CHUNK), BF),
            vmem((256, tok), BF),
            vmem((2, N_Z, 2, 256), BF),
            vmem((2, N_Z, 2, 256), BF),
            vmem((n_dp, 2, 256), F32),
            vmem((n_dp, 2, 256), F32),
            vmem((n_dp, 2, 256), F32),
            vmem((n_dp, 2, 256), F32),
            sem((4,)),
            sem((2, 2)),
            sem((2, 2)),
            sem((2, chunks)),
            sem((2, chunks)),
            sem((2,)),
            sem((2,)),
        ],
        compiler_params=pltpu.CompilerParams(collective_id=0, has_side_effects=True),
        name="monarch",
    )(tokens, right_weight, left_weight, cotangent)
    results = [pltpu.with_memory_space_constraint(r, pltpu.VMEM) for r in results]
    return pl.pallas_call(
        write_out,
        out_shape=[jax.ShapeDtypeStruct(*s) for s in shapes],
        in_specs=[in_vmem] * 3,
        out_specs=[any_space] * 3,
        scratch_shapes=[sem((3,))],
        name="write_out",
    )(*results)


def solution(mesh):
    return jax.shard_map(
        shards,
        mesh=mesh,
        in_specs=(P("dp", "mp"), P("mp", "dp", None), P("mp", "dp", None), P("dp", "mp")),
        out_specs=(P("dp", "mp"), P("mp", "dp", None), P("mp", "dp", None)),
        check_vma=False,
    )
```

time: 54.4 us -> 50.7 us (0.932)
  local copies, waits for them, and re-layouts: 3.15 us -> 0 us
  Pallas kernels: 50.5 us -> 49.9 us
    unnamed x7 -> x0, local copies, waits for them, and re-layouts: 3.15 us -> none
    pallas_call x1 -> x2, Pallas kernels: 50.5 us -> 49.9 us  [the longest x1 49.1 us: shards(): pl.pallas_call(kernel, out_shape=[pltpu.VMEM(*s) for s in shapes], in_spe...]
where the time goes in v2:
time: 50.7 us; the launch traced here: 50.6 us
  Pallas kernels  49.9 us (98%)
  between operations  0.64 us (1%)
    pallas_call x1, Pallas kernels, shards(): pl.pallas_call(kernel, out_shape=[pltpu.VMEM(*s) for s in shapes], in_spe...  49.1 us

profile of v2, /device:TPU:1, one launch (start us, length us, event | category | flops | bytes accessed | tf_op | source)
XLA Modules:
  0.0 50.6 jit_solution(17436938851986036920)
XLA Ops:
  0.6 49.1 %monarch.1 = (bf16[1024,256]{1,0:T(8,128)(2,1)S(1)}, f32[4,2,64]{2,1,0:T(2,128)S(1)}, f32[4,2,64]{2,1,0:T(2,128)S(1)}) custom-call(bf16[1024,256]{1,0:T(8,128)(2,1)} %x_hbm.1, bf16[4,2,64]{2,1,0:T(2,128)(2,1)} %rw_hbm.1, bf16[4,2,64]{2,1,0:T(2,128)(2,1)} %lw_hbm.1, bf16[1024,256]{1,0:T(8,128)(2,1)} %cot_hbm.1), custom_call_target="tpu_custom_call" | custom-call | tf_op jit(solution)/shard_map/monarch/pallas_call | solution.py:285
  49.7 0.8 %write_out.1 = (bf16[1024,256]{1,0:T(8,128)(2,1)}, f32[4,2,64]{2,1,0:T(2,128)}, f32[4,2,64]{2,1,0:T(2,128)}) custom-call(bf16[1024,256]{1,0:T(8,128)(2,1)S(1)} %get-tuple-element.6.act, f32[4,2,64]{2,1,0:T(2,128)S(1)} %get-tuple-element.7.gr, f32[4,2,64]{2,1,0:T(2,128)S(1)} %get-tuple-element.8.gl), custom_call_target="tpu_custom_call" | custom-call | tf_op jit(solution)/shard_map/write_out/pallas_call | solution.py:320
